TPU v7x, 32 devices: a whole 2x2x4 slice. The times are simulated.
32 devices in a mesh: gx: 4 (over z), gy: 8 (over y, x, core).
Axes of the slice: x: 2, y: 2, z: 4, core: 2. Of those that a mesh axis runs over, the one named last changes fastest.
Arguments:
- gradient: float32 [32, 2048], P('gx', 'gy'), may hold values from -6 to 6
- warm_start: float32 [32, 2048], P('gx', 'gy'), may hold values from -3 to 3
- viscosity: float32 [32, 32, 2048], P(None, 'gx', 'gy'), may hold values from 1 to 10
- friction_coef: float32 [32, 2048], P('gx', 'gy'), may hold values from 0.5 to 5
- slide_dir: float32 [2, 32, 2048], P(None, 'gx', 'gy'), may hold values from -4 to 4
- obs_weight: float32 [32, 2048], P('gx', 'gy'), may hold values from 0.5 to 2
- ice_mask: int32 [32, 2048], P('gx', 'gy'), may hold values 0 or 1
- grounded: int32 [32, 2048], P('gx', 'gy'), may hold values 0 or 1
Outputs:
- solution: float32 [32, 2048], P('gx', 'gy')
- residual: float32 [32, 2048], P('gx', 'gy')
All inputs are finite; a program needn't handle non-finite values. No bound on the sum of `ice_mask` or of `grounded` on one device may be relied on, other than what follows from the above.
Results may differ from a plain program's by a relative error of at most 0.00075.
Values sent between devices are 32-bit elements; how exact they have to be, the bound alone decides.
A program may use at most 128 MiB of HBM per device.

v0:
```python
import functools

import jax
import jax.numpy as jnp
from jax import lax
from jax.experimental import pallas as pl
from jax.experimental.pallas import tpu as pltpu
from jax.sharding import PartitionSpec as P

vert_coupling = 128.0
sink_rate = 0.0625
bed_drag = 0.5
offset_weight = 0.0019
cross_share = 0.5
reg_gamma = 0.02
reg_smooth = 1.0
diag_scale = 0.003

MESH = pl.DeviceIdType.MESH
REACH = 6
DIRS = [(-1, 0), (1, 0), (0, -1), (0, 1), (-1, -1), (-1, 1), (1, -1), (1, 1)]
OPPOSITE = [1, 0, 3, 2, 7, 6, 5, 4]
FIELDS = 7


def roll(x, shift, axis):
    size = x.shape[axis]
    if isinstance(shift, int):
        shift = shift % size
        if shift == 0:
            return x
    return pltpu.roll(x, shift, axis)


def near(x, step, axis):
    return roll(x, -step, axis)


def kernel(
    nx, ny,
    grad_in, warm_in, visc_in, fric_in, slide_in, obs_in, ice_in, ground_in,
    out_ref,
    grad_ref, warm_ref, visc_ref, fric_ref, slide_ref, obs_ref, ice_ref, ground_ref,
    up, down, bot, gbot, top, gtop,
    t_row, row_send, row_recv, f_send, f_recv, p_send, p_recv, k_send, k_recv, kp_send, kp_recv,
    ext, red, slots,
    load_sem, s_send, s_recv, r_send, r_recv, all_in,
):
    levels, rows, cols = visc_ref.shape
    n = nx * ny
    ix, iy = lax.axis_index("gx"), lax.axis_index("gy")
    me = ix * ny + iy

    loads = [
        pltpu.make_async_copy(src, dst, load_sem.at[j])
        for j, (src, dst) in enumerate((
            (visc_in, visc_ref), (fric_in, fric_ref), (ground_in, ground_ref), (ice_in, ice_ref),
            (slide_in, slide_ref), (obs_in, obs_ref), (warm_in, warm_ref), (grad_in, grad_ref),
        ))
    ]

    def exists(d):
        dx, dy = DIRS[d]
        x, y = ix + dx, iy + dy
        return (x >= 0) & (x < nx) & (y >= 0) & (y < ny)

    barrier = pltpu.get_barrier_semaphore()

    def greet(x, y):
        pl.semaphore_signal(barrier, inc=1, device_id=(x, y), device_id_type=MESH)

    for load in loads:
        load.start()
    expected = nx - 1 + ny - 1
    for d in range(4, 8):
        expected = expected + exists(d).astype(jnp.int32)

        @pl.when(exists(d))
        def _():
            greet(ix + DIRS[d][0], iy + DIRS[d][1])
    for k in range(1, nx):
        greet(lax.rem(ix + k, nx), iy)
    for k in range(1, ny):
        greet(ix, lax.rem(iy + k, ny))

    def copy(src, dst, d, sem):
        dx, dy = DIRS[d]
        return pltpu.make_async_remote_copy(
            src_ref=src, dst_ref=dst,
            send_sem=s_send.at[sem + d], recv_sem=s_recv.at[sem + OPPOSITE[d]],
            device_id=(jnp.clip(ix + dx, 0, nx - 1), jnp.clip(iy + dy, 0, ny - 1)),
            device_id_type=MESH,
        )

    def message(d, what):
        o = OPPOSITE[d]
        side = 0 if DIRS[d][1] < 0 else 1
        return {
            "row": lambda: copy(row_send.at[d], row_recv.at[o], d, 0),
            "field": lambda: copy(f_send, f_recv.at[o], d, 8),
            "coef": lambda: copy(k_send, k_recv.at[o], d, 16),
            "pack": lambda: copy(p_send.at[side], p_recv.at[o - 2], d, 0),
            "coefpack": lambda: copy(kp_send.at[side], kp_recv.at[o - 2], d, 16),
        }[what]()

    beside_x, others = (0, 1), range(2, 8)
    kinds = (("row", beside_x), ("pack", others), ("field", beside_x), ("coefpack", others), ("coef", beside_x))

    def each(action, names):
        for name, towards in kinds:
            if name not in names:
                continue
            for d in towards:
                @pl.when(exists(d))
                def _():
                    if action == "wait_recv":
                        message(OPPOSITE[d], name).wait_recv()
                    elif action == "wait_send":
                        message(d, name).wait_send()
                    else:
                        message(d, name).start()

    def clear(ref):
        ref[...] = jnp.zeros(ref.shape, jnp.float32)

    for d in range(8):
        @pl.when(jnp.logical_not(exists(d)))
        def _():
            for ref in (row_recv, f_recv, k_recv) if d < 2 else (p_recv, kp_recv):
                clear(ref.at[d if d < 2 else d - 2])

    for load in loads:
        load.wait()

    ice = ice_ref[...].astype(jnp.float32)
    ground = ground_ref[...].astype(jnp.float32)
    fric = fric_ref[...]
    friction = ground * fric
    base = ice * ground * fric
    inverse = 1.0 / (reg_gamma * (1.0 + 4.0 * reg_smooth) + diag_scale * base * fric)
    lane = lax.broadcasted_iota(jnp.int32, (rows, 128), 1)

    def eliminate(i, carry):
        e, f = carry
        k = levels - 2 - i
        v_low, v_up = visc_ref[i], visc_ref[i + 1]
        link = (vert_coupling * 0.5) * (v_low + v_up)
        ratio = link / (link + e)
        up[i] = ratio
        e = sink_rate * v_up + e * ratio
        w_low, w_up = visc_ref[k], visc_ref[k + 1]
        link = (vert_coupling * 0.5) * (w_low + w_up)
        ratio = link / (link + f)
        down[k] = ratio
        f = sink_rate * w_low + f * ratio
        return e, f

    e = sink_rate * visc_ref[0] + bed_drag * friction
    f = sink_rate * visc_ref[levels - 1]
    e, f = lax.fori_loop(0, levels - 1, eliminate, (e, f), unroll=True)

    zero = jnp.zeros((rows, cols), jnp.float32)
    for ref in (top, gtop):
        ref[0] = zero
        ref[levels + 1] = zero

    def respond(z, carry):
        b, t, left, right, tleft, tright = carry
        g = visc_ref[z] * b
        bot[z] = b
        gbot[z] = g
        for j, val in ((0, b), (levels, g)):
            row_send[0, pl.ds(z + j, 1), :] = val[:1]
            row_send[1, pl.ds(z + j, 1), :] = val[rows - 1:]
            left = jnp.where(lane == z + j, roll(val[:, :128], z + j, 1), left)
            right = jnp.where(lane == z + j, roll(val[:, cols - 128:], z + j + 1, 1), right)
        k = levels - 1 - z
        top[k + 1] = t
        h = visc_ref[k] * t
        gtop[k + 1] = h
        for j, val in ((0, h), (levels, t)):
            t_row[0, pl.ds(k + j, 1), :] = val[:1]
            t_row[1, pl.ds(k + j, 1), :] = val[rows - 1:]
            tleft = jnp.where(lane == k + j, roll(val[:, :128], k + j, 1), tleft)
            tright = jnp.where(lane == k + j, roll(val[:, cols - 128:], k + j + 1, 1), tright)
        t = t * up[jnp.maximum(k - 1, 0)]
        b = b * down[jnp.minimum(z, levels - 2)]
        return b, t, left, right, tleft, tright

    blank = jnp.zeros((rows, 128), jnp.float32)
    _, _, left, right, tleft, tright = lax.fori_loop(
        0, levels, respond, (1.0 / (f + bed_drag * friction), 1.0 / e, blank, blank, blank, blank), unroll=4
    )

    own = [base * slide_ref[0], base * slide_ref[1], ice * obs_ref[...], inverse, bot[levels - 1], warm_ref[...], grad_ref[...]]

    def pack(fields, place, left, right):
        for val in fields:
            here = (lane >= place) & (lane < place + REACH)
            left = jnp.where(here, roll(val[:, :128], place, 1), left)
            right = jnp.where(here, roll(val[:, cols - 128:], place - (128 - REACH), 1), right)
            place += REACH
        return left, right

    left, right = pack(own, 2 * levels, left, right)
    for j, val in enumerate(own):
        f_send[j] = val
    p_send[0] = left
    p_send[1] = right

    pl.semaphore_wait(barrier, expected)
    each("start", ("row", "pack", "field"))
    for k in range(1, ny):
        pl.semaphore_signal(all_in, inc=1, device_id=(ix, lax.rem(iy + k, ny)), device_id_type=MESH)

    row_id = lax.broadcasted_iota(jnp.int32, (rows, cols), 0)
    col_id = lax.broadcasted_iota(jnp.int32, (rows, cols), 1)
    prow = lax.broadcasted_iota(jnp.int32, (rows, 128), 0)

    def beside(side):
        at = {dx: p_recv[DIRS.index((dx, side)) - 2] for dx in (-1, 0, 1)}
        return {
            -1: jnp.where(prow == 0, near(at[-1], -1, 0), near(at[0], -1, 0)),
            0: at[0],
            1: jnp.where(prow == rows - 1, near(at[1], 1, 0), near(at[0], 1, 0)),
        }

    def weigh(mid, out):
        return (
            (0.5 * offset_weight) * mid + (0.25 * offset_weight) * out,
            (0.25 * offset_weight) * mid + (0.5 * offset_weight / 3.0) * out,
        )

    def gather(z, acc):
        acc = list(acc)
        weights = [weigh(ref[z + 1], ref[z] + ref[z + 2]) for ref in (gtop, top)]
        for ref, weight in ((bot, weights[0]), (gbot, weights[1])):
            mid = ref[z]
            low = jnp.where(row_id == 0, 0.0, near(mid, -1, 0))
            high = jnp.where(row_id == rows - 1, 0.0, near(mid, 1, 0))
            for dx, val in ((-1, low), (0, mid), (1, high)):
                for dy in (-1, 0, 1):
                    if (dx, dy) != (0, 0):
                        d = DIRS.index((dx, dy))
                        moved = val if dy == 0 else near(val, dy, 1)
                        acc[d] = acc[d] + weight[1 if dx * dy != 0 else 0] * moved
        return tuple(acc)

    coefs = list(lax.fori_loop(0, levels, gather, (zero,) * 8, unroll=4))
    for d, (dx, dy) in enumerate(DIRS):
        if dy != 0:
            coefs[d] = jnp.where(col_id == (0 if dy < 0 else cols - 1), 0.0, coefs[d])

    layer = lax.broadcasted_iota(jnp.int32, (2 * levels, cols), 0)
    edge_col = lax.broadcasted_iota(jnp.int32, (2 * levels, cols), 1)

    def above_below(mid, index, axis):
        low = (index == 0) | (index == levels) | (index >= 2 * levels)
        high = (index == levels - 1) | (index >= 2 * levels - 1)
        return jnp.where(low, 0.0, near(mid, -1, axis)) + jnp.where(high, 0.0, near(mid, 1, axis))

    row_weights = [weigh(t_row[i], above_below(t_row[i], layer, 0)) for i in (0, 1)]
    col_weights = [weigh(t, above_below(t, lane, 1)) for t in (tleft, tright)]
    each("wait_recv", ("row", "pack"))
    for i, dx in enumerate((-1, 1)):
        halo = row_recv[i]
        for dy in (-1, 0, 1):
            d = DIRS.index((dx, dy))
            val = halo
            if dy != 0:
                val = jnp.where(edge_col == (0 if dy < 0 else cols - 1), 0.0, near(halo, dy, 1))
            part = jnp.sum(row_weights[i][1 if dy != 0 else 0] * val, axis=0, keepdims=True)
            coefs[d] = coefs[d] + jnp.where(row_id == (0 if dx < 0 else rows - 1), part, 0.0)
    for i, dy in enumerate((-1, 1)):
        at = beside(dy)
        for dx in (-1, 0, 1):
            d = DIRS.index((dx, dy))
            part = jnp.sum(col_weights[i][1 if dx != 0 else 0] * at[dx], axis=1, keepdims=True)
            coefs[d] = coefs[d] + jnp.where(col_id == (0 if dy < 0 else cols - 1), part, 0.0)
    for d in range(8):
        k_send[d] = coefs[d]
    kleft, kright = pack(coefs, 0, blank, blank)
    kp_send[0] = kleft
    kp_send[1] = kright
    each("start", ("coefpack", "coef"))

    def extend(j, mine, recv, packs_ref, index, place):
        for tile, dx in enumerate((-1, 0, 1)):
            here = mine if dx == 0 else recv[0 if dx < 0 else 1, index]
            from_right = packs_ref[DIRS.index((dx, 1)) - 2]
            from_left = packs_ref[DIRS.index((dx, -1)) - 2]
            halo = jnp.where(lane < REACH, roll(from_right, -place, 1), 0.0)
            halo = jnp.where(lane >= 128 - REACH, roll(from_left, 128 - REACH - place, 1), halo)
            ext[j, tile * rows:(tile + 1) * rows, :cols] = here
            ext[j, tile * rows:(tile + 1) * rows, cols:] = halo

    each("wait_recv", ("field",))
    for j in range(FIELDS):
        extend(j, f_send[j], f_recv, p_recv, j, 2 * levels + REACH * j)
    each("wait_recv", ("coefpack", "coef"))
    for d in range(8):
        extend(FIELDS + d, k_send[d], k_recv, kp_recv, d, REACH * d)

    def coef(dx, dy):
        return ext[FIELDS + DIRS.index((dx, dy))]

    def forth(q):
        spread = [ext[0] * q, ext[1] * q]
        surface = [ext[4] * spread[0], ext[4] * spread[1]]
        for dx in (-1, 0, 1):
            moved = [near(s, dx, 0) for s in spread]
            for dy in (-1, 0, 1):
                if (dx, dy) == (0, 0):
                    continue
                share = cross_share * dx * dy
                for c in range(2):
                    val = moved[c] if share == 0 else moved[c] + share * moved[1 - c]
                    surface[c] = surface[c] + coef(dx, dy) * near(val, dy, 1)
        return surface

    def back(q, surface):
        traction = [ext[2] * s for s in surface]
        basal = [ext[4] * t for t in traction]
        for dx in (-1, 0, 1):
            part = [None, None]
            for dy in (-1, 0, 1):
                if (dx, dy) == (0, 0):
                    continue
                share = cross_share * dx * dy
                for c in range(2):
                    val = traction[c] if share == 0 else traction[c] + share * traction[1 - c]
                    val = near(coef(-dx, -dy) * val, dy, 1)
                    part[c] = val if part[c] is None else part[c] + val
            basal = [basal[c] + near(part[c], dx, 0) for c in range(2)]
        return ext[0] * basal[0] + ext[1] * basal[1] + regularize(q)

    def regularize(q):
        around = near(q, 1, 0) + near(q, -1, 0) + near(q, 1, 1) + near(q, -1, 1)
        return reg_gamma * (q + reg_smooth * (4.0 * q - around))

    def hessian(q):
        return back(q, forth(q))

    def mine(x):
        return x[rows:2 * rows, :cols]

    warm = ext[5]
    image = hessian(warm)
    r0 = ext[6] - image
    p0 = ext[3] * r0
    w0 = hessian(p0)
    y0 = ext[3] * w0
    surface = forth(y0)
    curve0 = mine(ext[2]) * (mine(surface[0]) * mine(surface[0]) + mine(surface[1]) * mine(surface[1])) + mine(y0 * regularize(y0))
    full_y0 = y0
    r0, p0, w0, y0 = mine(r0), mine(p0), mine(w0), mine(y0)

    def total(x):
        return jnp.sum(jnp.sum(x, axis=0, keepdims=True), axis=1, keepdims=True)

    one_lane = lax.broadcasted_iota(jnp.int32, (1, 128), 1)
    sums = jnp.zeros((1, 128), jnp.float32)
    for j, val in enumerate((r0 * p0, p0 * w0, w0 * y0, curve0)):
        sums = jnp.where(one_lane == j, total(val), sums)
    red[...] = sums

    def to_peer(j, index):
        peer = lax.rem(me + j, n)
        return pltpu.make_async_remote_copy(
            src_ref=red, dst_ref=slots.at[index],
            send_sem=r_send.at[j], recv_sem=r_recv.at[index],
            device_id=(peer // ny, lax.rem(peer, ny)), device_id_type=MESH,
        )

    def send(j, c):
        to_peer(j, me).start()
        return c

    def receive(j, c):
        to_peer(j, lax.rem(me + j, n)).wait_recv()
        return c

    def sent(j, c):
        to_peer(j, me).wait_send()
        return c

    pl.semaphore_wait(all_in, ny - 1)
    lax.fori_loop(1, n, send, 0, unroll=4)
    u0 = mine(back(full_y0, surface))
    each("wait_send", [name for name, _ in kinds])
    lax.fori_loop(1, n, receive, 0, unroll=4)
    slots[me] = sums
    everyone = jnp.sum(slots[...], axis=0)

    def pick(j):
        return jnp.sum(jnp.where(one_lane == j, everyone, 0.0), axis=1, keepdims=True)

    rz0, pw, wy, yu = pick(0), pick(1), pick(2), pick(3)
    a0 = rz0 / pw
    rz1 = a0 * a0 * wy - rz0
    beta = rz1 / rz0
    more = 1.0 + beta
    curve = more * (more * pw - 2.0 * a0 * wy) + a0 * a0 * yu
    a1 = rz1 / curve
    out_ref[0] = a0 * p0 + a1 * (more * p0 - a0 * y0)
    out_ref[1] = -mine(image) - a0 * w0 - a1 * (more * w0 - a0 * u0)
    lax.fori_loop(1, n, sent, 0)


def solution(mesh):
    nx, ny = mesh.shape["gx"], mesh.shape["gy"]
    n = nx * ny

    def on_device(gradient, warm_start, viscosity, friction_coef, slide_dir, obs_weight, ice_mask, grounded):
        levels, rows, cols = viscosity.shape
        vmem = pl.BlockSpec(memory_space=pltpu.VMEM)
        f32 = lambda *shape: pltpu.VMEM(shape, jnp.float32)
        flat = (gradient, warm_start, viscosity, friction_coef, slide_dir, obs_weight, ice_mask, grounded)
        change = pl.pallas_call(
            functools.partial(kernel, nx, ny),
            out_shape=jax.ShapeDtypeStruct((2, rows, cols), jnp.float32),
            in_specs=[pl.BlockSpec(memory_space=pl.ANY)] * 8,
            out_specs=vmem,
            scratch_shapes=[
                *(pltpu.VMEM(a.shape, a.dtype) for a in flat),
                f32(levels, rows, cols), f32(levels, rows, cols),
                f32(levels, rows, cols), f32(levels, rows, cols),
                f32(levels + 2, rows, cols), f32(levels + 2, rows, cols),
                f32(2, 2 * levels, cols), f32(2, 2 * levels, cols), f32(2, 2 * levels, cols),
                f32(FIELDS, rows, cols), f32(2, FIELDS, rows, cols),
                f32(2, rows, 128), f32(6, rows, 128),
                f32(8, rows, cols), f32(2, 8, rows, cols),
                f32(2, rows, 128), f32(6, rows, 128),
                f32(FIELDS + 8, 3 * rows, cols + 128),
                f32(1, 128), f32(n, 1, 128),
                pltpu.SemaphoreType.DMA((8,)),
                pltpu.SemaphoreType.DMA((24,)), pltpu.SemaphoreType.DMA((24,)),
                pltpu.SemaphoreType.DMA((n,)), pltpu.SemaphoreType.DMA((n,)),
                pltpu.SemaphoreType.REGULAR,
            ],
            compiler_params=pltpu.CompilerParams(collective_id=0, has_side_effects=True),
        )(*flat)
        return warm_start + change[0], gradient + change[1]

    flat = P("gx", "gy")
    deep = P(None, "gx", "gy")
    return jax.shard_map(
        on_device,
        mesh=mesh,
        in_specs=(flat, flat, deep, flat, deep, flat, flat, flat),
        out_specs=(flat, flat),
        check_vma=False,
    )
```

profile of v0, /device:TPU:0, one launch (start us, length us, event | category | flops | bytes accessed | tf_op | source)
XLA Modules:
  0.0 23.5 jit_solution(10367176348225715624)
XLA Ops:
  0.6 0.0 copy-start.1
  0.6 0.0 copy-start
  0.7 21.5 %shard_map.95 = f32[2,8,256]{2,1,0:T(8,128)} custom-call(f32[8,256]{1,0:T(8,128)} %grad_in.1, f32[8,256]{1,0:T(8,128)} %warm_in.1, f32[32,8,256]{2,1,0:T(8,128)} %visc_in.1, f32[8,256]{1,0:T(8,128)} %fric_in.1, f32[2,8,256]{2,1,0:T(8,128)} %slide_in.1, f32[8,256]{1,0:T(8,128)} %obs_in.1, s32[8,256]{1,0:T(8,128)} %ice_in.1, s32[8,256]{1,0:T(8,128)} %ground_in.1), custom_call_target="tpu_custom_call" | custom-call | tf_op jit(solution)/shard_map/pallas_call | solution.py:419
  22.2 0.0 copy-done.1
  22.2 0.0 copy-done
  22.2 1.3 %bitcast_add_fusion = (f32[8,256]{1,0:T(8,128)}, f32[8,256]{1,0:T(8,128)}) fusion(f32[8,256]{1,0:T(8,128)S(1)} %copy-done, f32[2,8,256]{2,1,0:T(8,128)} %shard_map.95, f32[8,256]{1,0:T(8,128)S(1)} %copy-done.1), kind=kLoop, calls=%fused_computation | loop fusion | flops 4096 | bytes 49152 | tf_op jit(solution)/shard_map/add | solution.py:443
Async XLA Ops:
  0.6 21.6 %copy-start.1 = (f32[8,256]{1,0:T(8,128)S(1)}, f32[8,256]{1,0:T(8,128)}, u32[]{:S(2)}) copy-start(f32[8,256]{1,0:T(8,128)} %warm_in.1) | copy-start | bytes 24580
  0.6 21.6 %copy-start = (f32[8,256]{1,0:T(8,128)S(1)}, f32[8,256]{1,0:T(8,128)}, u32[]{:S(2)}) copy-start(f32[8,256]{1,0:T(8,128)} %grad_in.1) | copy-start | bytes 24580
where the time goes:
time: 23.7 us; the launch traced here: 23.5 us
  Pallas kernels  21.5 us (91%)
  other arithmetic  1.32 us (6%)
  between operations  0.67 us (3%)
    pallas_call x1, Pallas kernels, on_device(): pl.pallas_call(functools.partial(kernel, nx, ny), out_shape=jax.ShapeDtyp...  21.5 us
    add x1, other arithmetic, on_device(): return (warm_start + change[0], gradient + change[1])  1.32 us

commit v1 on v0

--- a/solution.py
+++ b/solution.py
@@ -17,6 +17,7 @@
 diag_scale = 0.003
 
 MESH = pl.DeviceIdType.MESH
+LOGICAL = pl.DeviceIdType.LOGICAL
 REACH = 6
 DIRS = [(-1, 0), (1, 0), (0, -1), (0, 1), (-1, -1), (-1, 1), (1, -1), (1, 1)]
 OPPOSITE = [1, 0, 3, 2, 7, 6, 5, 4]
@@ -364,31 +365,30 @@
         sums = jnp.where(one_lane == j, total(val), sums)
     red[...] = sums
 
-    def to_peer(j, index):
-        peer = lax.rem(me + j, n)
+    def to_peer(peer):
         return pltpu.make_async_remote_copy(
-            src_ref=red, dst_ref=slots.at[index],
-            send_sem=r_send.at[j], recv_sem=r_recv.at[index],
-            device_id=(peer // ny, lax.rem(peer, ny)), device_id_type=MESH,
+            src_ref=red, dst_ref=slots.at[me], send_sem=r_send, recv_sem=r_recv,
+            device_id=peer, device_id_type=LOGICAL,
         )
 
+    everybody = pltpu.make_async_remote_copy(
+        src_ref=slots.at[pl.ds(0, n - 1)], dst_ref=slots.at[pl.ds(0, n - 1)], send_sem=r_send, recv_sem=r_recv,
+        device_id=me, device_id_type=LOGICAL,
+    )
+
     def send(j, c):
-        to_peer(j, me).start()
+        peer = lax.rem(2 * n - 1 - me + j, n)
+
+        @pl.when(peer != me)
+        def _():
+            to_peer(peer).start()
         return c
 
-    def receive(j, c):
-        to_peer(j, lax.rem(me + j, n)).wait_recv()
-        return c
-
-    def sent(j, c):
-        to_peer(j, me).wait_send()
-        return c
-
     pl.semaphore_wait(all_in, ny - 1)
-    lax.fori_loop(1, n, send, 0, unroll=4)
+    lax.fori_loop(0, n, send, 0, unroll=8)
     u0 = mine(back(full_y0, surface))
     each("wait_send", [name for name, _ in kinds])
-    lax.fori_loop(1, n, receive, 0, unroll=4)
+    everybody.wait_recv()
     slots[me] = sums
     everyone = jnp.sum(slots[...], axis=0)
 
@@ -402,9 +402,9 @@
     more = 1.0 + beta
     curve = more * (more * pw - 2.0 * a0 * wy) + a0 * a0 * yu
     a1 = rz1 / curve
-    out_ref[0] = a0 * p0 + a1 * (more * p0 - a0 * y0)
-    out_ref[1] = -mine(image) - a0 * w0 - a1 * (more * w0 - a0 * u0)
-    lax.fori_loop(1, n, sent, 0)
+    out_ref[0] = warm_ref[...] + (a0 * p0 + a1 * (more * p0 - a0 * y0))
+    out_ref[1] = grad_ref[...] + (-mine(image) - a0 * w0 - a1 * (more * w0 - a0 * u0))
+    everybody.wait_send()
 
 
 def solution(mesh):
@@ -416,9 +416,9 @@
         vmem = pl.BlockSpec(memory_space=pltpu.VMEM)
         f32 = lambda *shape: pltpu.VMEM(shape, jnp.float32)
         flat = (gradient, warm_start, viscosity, friction_coef, slide_dir, obs_weight, ice_mask, grounded)
-        change = pl.pallas_call(
+        out = pl.pallas_call(
             functools.partial(kernel, nx, ny),
-            out_shape=jax.ShapeDtypeStruct((2, rows, cols), jnp.float32),
+            out_shape=f32(2, rows, cols),
             in_specs=[pl.BlockSpec(memory_space=pl.ANY)] * 8,
             out_specs=vmem,
             scratch_shapes=[
@@ -435,12 +435,12 @@
                 f32(1, 128), f32(n, 1, 128),
                 pltpu.SemaphoreType.DMA((8,)),
                 pltpu.SemaphoreType.DMA((24,)), pltpu.SemaphoreType.DMA((24,)),
-                pltpu.SemaphoreType.DMA((n,)), pltpu.SemaphoreType.DMA((n,)),
+                pltpu.SemaphoreType.DMA, pltpu.SemaphoreType.DMA,
                 pltpu.SemaphoreType.REGULAR,
             ],
             compiler_params=pltpu.CompilerParams(collective_id=0, has_side_effects=True),
         )(*flat)
-        return warm_start + change[0], gradient + change[1]
+        return out[0], out[1]
 
     flat = P("gx", "gy")
     deep = P(None, "gx", "gy")

time: 23.7 us -> 21.7 us (0.916)
  other arithmetic: 1.32 us -> 0 us
  Pallas kernels: 21.5 us -> 20.3 us
  local copies, waits for them, and re-layouts: 0.01 us -> 0.61 us
    add x1 -> x0, other arithmetic: 1.32 us -> none  [on_device(): return (warm_start + change[0], gradient + change[1])]
    pallas_call x1, Pallas kernels: 21.5 us -> 20.3 us  [on_device(): pl.pallas_call(functools.partial(kernel, nx, ny), out_shape=f32(2, rows,...]
    squeeze x0 -> x1, local copies, waits for them, and re-layouts: none -> 0.61 us  [on_device(): return (out[0], out[1])]
where the time goes in v1:
time: 21.7 us; the launch traced here: 21.6 us
  Pallas kernels  20.3 us (94%)
  between operations  0.64 us (3%)
  local copies, waits for them, and re-layouts  0.61 us (3%)
    pallas_call x1, Pallas kernels, on_device(): pl.pallas_call(functools.partial(kernel, nx, ny), out_shape=f32(2, rows,...  20.3 us
    squeeze x1, local copies, waits for them, and re-layouts, on_device(): return (out[0], out[1])  0.61 us

profile of v1, /device:TPU:0, one launch (start us, length us, event | category | flops | bytes accessed | tf_op | source)
XLA Modules:
  0.0 21.6 jit_solution(15592980326701609787)
XLA Ops:
  0.6 20.3 %shard_map.95 = f32[2,8,256]{2,1,0:T(8,128)S(1)} custom-call(f32[8,256]{1,0:T(8,128)} %grad_in.1, f32[8,256]{1,0:T(8,128)} %warm_in.1, f32[32,8,256]{2,1,0:T(8,128)} %visc_in.1, f32[8,256]{1,0:T(8,128)} %fric_in.1, f32[2,8,256]{2,1,0:T(8,128)} %slide_in.1, f32[8,256]{1,0:T(8,128)} %obs_in.1, s32[8,256]{1,0:T(8,128)} %ice_in.1, s32[8,256]{1,0:T(8,128)} %ground_in.1), custom_call_target="tpu_custom_call" | custom-call | tf_op jit(solution)/shard_map/pallas_call | solution.py:419
  21.0 0.6 %slice_bitcast_fusion = (f32[8,256]{1,0:T(8,128)}, f32[8,256]{1,0:T(8,128)}) fusion(f32[2,8,256]{2,1,0:T(8,128)S(1)} %shard_map.95), kind=kLoop, calls=%fused_computation | loop fusion | bytes 32768 | tf_op jit(solution)/shard_map/squeeze | solution.py:443

commit v2 on v1

v2 whole, which is shorter than its diff:
```python
import functools

import jax
import jax.numpy as jnp
from jax import lax
from jax.experimental import pallas as pl
from jax.experimental.pallas import tpu as pltpu
from jax.sharding import PartitionSpec as P

vert_coupling = 128.0
sink_rate = 0.0625
bed_drag = 0.5
offset_weight = 0.0019
cross_share = 0.5
reg_gamma = 0.02
reg_smooth = 1.0
diag_scale = 0.003

MESH = pl.DeviceIdType.MESH
LOGICAL = pl.DeviceIdType.LOGICAL
REACH = 6
DIRS = [(-1, 0), (1, 0), (0, -1), (0, 1), (-1, -1), (-1, 1), (1, -1), (1, 1)]
OPPOSITE = [1, 0, 3, 2, 7, 6, 5, 4]
BASE = 6


def roll(x, shift, axis):
    size = x.shape[axis]
    if isinstance(shift, int):
        shift = shift % size
        if shift == 0:
            return x
    return pltpu.roll(x, shift, axis)


def near(x, step, axis):
    return roll(x, -step, axis)


def kernel(
    nx, ny,
    grad_in, warm_in, visc_in, fric_in, slide_in, obs_in, ice_in, ground_in,
    out_ref,
    grad_ref, warm_ref, visc_ref, fric_ref, slide_ref, obs_ref, ice_ref, ground_ref,
    up, down, bot, gbot, top, gtop,
    vx, upx, downx, bx, gx, tx, hx,
    e_send, ef, a_send, a_recv, c_send, c_recv, k_send, k_recv,
    pk_send, pk_recv, px_recv, q_send, q_recv,
    ext, red, slots,
    load_sem, s_send, s_recv, r_send, r_recv, all_in,
):
    levels, rows, cols = visc_ref.shape
    n = nx * ny
    ix, iy = lax.axis_index("gx"), lax.axis_index("gy")
    me = ix * ny + iy

    loads = [
        pltpu.make_async_copy(src, dst, load_sem.at[j])
        for j, (src, dst) in enumerate((
            (visc_in, visc_ref), (fric_in, fric_ref), (ground_in, ground_ref), (ice_in, ice_ref),
            (slide_in, slide_ref), (obs_in, obs_ref), (warm_in, warm_ref), (grad_in, grad_ref),
        ))
    ]

    def exists(d):
        dx, dy = DIRS[d]
        x, y = ix + dx, iy + dy
        return (x >= 0) & (x < nx) & (y >= 0) & (y < ny)

    barrier = pltpu.get_barrier_semaphore()

    def greet(x, y):
        pl.semaphore_signal(barrier, inc=1, device_id=(x, y), device_id_type=MESH)

    for load in loads:
        load.start()
    expected = nx - 1 + ny - 1
    for d in range(4, 8):
        expected = expected + exists(d).astype(jnp.int32)

        @pl.when(exists(d))
        def _():
            greet(ix + DIRS[d][0], iy + DIRS[d][1])
    for k in range(1, nx):
        greet(lax.rem(ix + k, nx), iy)
    for k in range(1, ny):
        greet(ix, lax.rem(iy + k, ny))

    def copy(src, dst, d, sem):
        dx, dy = DIRS[d]
        return pltpu.make_async_remote_copy(
            src_ref=src, dst_ref=dst,
            send_sem=s_send.at[sem + d], recv_sem=s_recv.at[sem + OPPOSITE[d]],
            device_id=(jnp.clip(ix + dx, 0, nx - 1), jnp.clip(iy + dy, 0, ny - 1)),
            device_id_type=MESH,
        )

    def message(d, what):
        o = OPPOSITE[d]
        dx, dy = DIRS[d]
        side = 0 if dy < 0 else 1

        def part(k):
            return pl.ds(0 if dx < 0 else rows - k, k)

        return {
            "pack": lambda: copy(pk_send.at[side], pk_recv.at[o - 2], d, 0),
            "visc": lambda: copy(visc_ref.at[:, part(1), :], vx.at[:, part(1), pl.ds(0, cols)], d, 0),
            "late": lambda: copy(q_send.at[side], q_recv.at[o - 2], d, 8),
            "edge": lambda: copy(e_send.at[:, part(1), :], ef.at[:, part(1), :], d, 8),
            "side": lambda: copy(pk_send.at[:, 0], px_recv.at[o], d, 16),
            "wide": lambda: copy(a_send.at[:, part(REACH), :], a_recv.at[o, :, part(REACH), :], d, 18),
            "less": lambda: copy(c_send.at[:, part(REACH - 2), :], c_recv.at[o, :, part(REACH - 2), :], d, 20),
            "coef": lambda: copy(k_send.at[:, part(REACH - 1), :], k_recv.at[o, :, part(REACH - 1), :], d, 22),
        }[what]()

    beside_x, others = (0, 1), range(2, 8)
    kinds = (
        ("pack", others), ("visc", beside_x), ("edge", beside_x), ("side", beside_x), ("wide", beside_x), ("less", beside_x),
        ("late", others), ("coef", beside_x),
    )

    def each(action, names):
        for name, towards in kinds:
            if name not in names:
                continue
            for d in towards:
                @pl.when(exists(d))
                def _():
                    if action == "wait_recv":
                        message(OPPOSITE[d], name).wait_recv()
                    elif action == "wait_send":
                        message(d, name).wait_send()
                    else:
                        message(d, name).start()

    def fill(ref, value=0.0):
        ref[...] = jnp.full(ref.shape, value, jnp.float32)

    for d in range(8):
        @pl.when(jnp.logical_not(exists(d)))
        def _():
            if d < 2:
                row = pl.ds(rows - 1 if d == 0 else 0, 1)
                fill(vx.at[:, row, pl.ds(0, cols)], 1.0)
                fill(ef.at[:, row, :])
                for ref in (px_recv, a_recv, c_recv, k_recv):
                    fill(ref.at[d])
            else:
                fill(pk_recv.at[d - 2, 0])
                fill(pk_recv.at[d - 2, 1], 1.0)
                fill(pk_recv.at[d - 2, 2])
                fill(q_recv.at[d - 2])

    for load in loads:
        load.wait()

    ice = ice_ref[...].astype(jnp.float32)
    ground = ground_ref[...].astype(jnp.float32)
    fric = fric_ref[...]
    friction = ground * fric
    base = ice * ground * fric
    inverse = 1.0 / (reg_gamma * (1.0 + 4.0 * reg_smooth) + diag_scale * base * fric)
    watch = ice * jnp.sqrt(obs_ref[...])
    turned = base * (0.5 ** 0.5)
    sum_src = turned * (slide_ref[0] + slide_ref[1])
    dif_src = turned * (slide_ref[0] - slide_ref[1])
    lane = lax.broadcasted_iota(jnp.int32, (rows, 128), 1)
    prow = lax.broadcasted_iota(jnp.int32, (rows, 128), 0)

    def factor(v, up, down, drag):
        def eliminate(i, carry):
            e, f = carry
            k = levels - 2 - i
            v_low, v_up = v[i], v[i + 1]
            link = (vert_coupling * 0.5) * (v_low + v_up)
            ratio = link / (link + e)
            up[i] = ratio
            e = sink_rate * v_up + e * ratio
            w_low, w_up = v[k], v[k + 1]
            link = (vert_coupling * 0.5) * (w_low + w_up)
            ratio = link / (link + f)
            down[k] = ratio
            f = sink_rate * w_low + f * ratio
            return e, f

        e = sink_rate * v[0] + drag
        f = sink_rate * v[levels - 1]
        e, f = lax.fori_loop(0, levels - 1, eliminate, (e, f), unroll=True)
        return e, f + drag

    def layer(z):
        return pl.ds(z * rows, rows)

    def put(ref, z, val):
        for c in range(val.shape[1] // 128):
            ref[c, layer(z), :] = val[:, c * 128:(c + 1) * 128]

    def get(ref, z):
        return jnp.concatenate([ref[c, layer(z), :] for c in range(ref.shape[0])], axis=1)

    e, f = factor(visc_ref, up, down, bed_drag * friction)
    zero = jnp.zeros((rows, cols), jnp.float32)
    for ref in (top, gtop):
        put(ref, 0, zero)
        put(ref, levels + 1, zero)

    blank = jnp.zeros((rows, 128), jnp.float32)
    half = levels // 2
    left, right = blank, blank
    near_left, near_right = [blank + 1.0] * 2, [blank + 1.0] * 2
    b, t = (0.25 * offset_weight) / f, watch / e
    for z in range(levels):
        k = levels - 1 - z
        v = visc_ref[z]
        g, h = v * b, visc_ref[k] * t
        put(bot, z, b)
        put(gbot, z, g)
        put(top, k + 1, t)
        put(gtop, k + 1, h)
        for place, val in ((z, b), (levels + z, g), (2 * levels + k, h), (3 * levels + k, t)):
            left = jnp.where(lane == place, roll(val[:, :128], place, 1), left)
            right = jnp.where(lane == place, roll(val[:, cols - 128:], place + 1, 1), right)
        place = REACH * (z % half)
        here = (lane >= place) & (lane < place + REACH)
        near_left[z // half] = jnp.where(here, roll(v[:, :128], place, 1), near_left[z // half])
        near_right[z // half] = jnp.where(here, roll(v[:, cols - 128:], place + REACH, 1), near_right[z // half])
        if z < levels - 1:
            t = t * up[k - 1]
            b = b * down[z]
    through = t

    def pack(fields, place, left, right):
        for val in fields:
            here = (lane >= place) & (lane < place + REACH)
            left = jnp.where(here, roll(val[:, :128], place, 1), left)
            right = jnp.where(here, roll(val[:, cols - 128:], place - (128 - REACH), 1), right)
            place += REACH
        return left, right

    for j, val in enumerate((sum_src, dif_src, warm_ref[...])):
        a_send[j] = val
    for j, val in enumerate((inverse, grad_ref[...])):
        c_send[j] = val
    k_send[0] = through
    for j, val in enumerate((friction, watch)):
        e_send[j] = val
    fields = pack((sum_src, dif_src, warm_ref[...], inverse, grad_ref[...], through, friction, watch), 0, blank, blank)
    folded = (prow == 1) | (prow == 2)
    for side, strip, sight in ((0, left, near_left), (1, right, near_right)):
        pk_send[side, 0] = strip
        pk_send[side, 1] = jnp.where(folded, roll(sight[1], 2, 0), sight[0])
        pk_send[side, 2] = fields[side]

    pl.semaphore_wait(barrier, expected)
    each("start", ("pack", "visc", "edge", "side", "wide", "less"))
    for k in range(1, ny):
        pl.semaphore_signal(all_in, inc=1, device_id=(ix, lax.rem(iy + k, ny)), device_id_type=MESH)

    def weigh(mid, out):
        return 2.0 * mid + out, mid + (2.0 / 3.0) * out

    def gather(z, acc):
        acc = list(acc)
        for ref, other in ((bot, gtop), (gbot, top)):
            straight, slant = weigh(get(other, z + 1), get(other, z) + get(other, z + 2))
            mid = get(ref, z)
            for dy, val in ((-1, near(mid, -1, 1)), (0, mid), (1, near(mid, 1, 1))):
                for dx in (-1, 0, 1):
                    if (dx, dy) != (0, 0):
                        d = DIRS.index((dx, dy))
                        weight = slant if dx * dy != 0 else straight
                        acc[d] = acc[d] + (weight if dx == 0 else near(weight, -dx, 0)) * val
        return tuple(acc)

    row_id = lax.broadcasted_iota(jnp.int32, (rows, cols), 0)
    col_id = lax.broadcasted_iota(jnp.int32, (rows, cols), 1)
    coefs = list(lax.fori_loop(0, levels, gather, (zero,) * 8, unroll=8))
    for d, (dx, dy) in enumerate(DIRS):
        if dx != 0:
            coefs[d] = jnp.where(row_id == (0 if dx < 0 else rows - 1), 0.0, near(coefs[d], dx, 0))
        if dy != 0:
            coefs[d] = jnp.where(col_id == (0 if dy < 0 else cols - 1), 0.0, coefs[d])
        k_send[1 + d] = coefs[d]
    q_send[0], q_send[1] = pack(coefs, 0, blank, blank)
    each("start", ("late", "coef"))

    def pick(packs, dx, dy):
        return packs[DIRS.index((dx, dy)) - 2]

    def corner(which, dy):
        flat = [pk_recv[DIRS.index((dx, dy)) - 2, which] for dx in (-1, 1)]
        return jnp.where((prow == 0) | (prow == 2), flat[1], flat[0])

    inner = (lane >= 32) & (lane < 96)
    after = lane < 64

    def frame(which):
        sides = [pk_recv[DIRS.index((0, dy)) - 2, which] for dy in (1, -1)]
        corners = [corner(which, dy) for dy in (1, -1)]

        def at(place):
            ahead = jnp.where(inner, roll(corners[0], 64 - place, 1), roll(sides[0], -place, 1))
            behind = jnp.where(inner, roll(corners[1], 64 - REACH - place, 1), roll(sides[1], -REACH - place, 1))
            return jnp.where(inner, jnp.where(lane < 64, behind, ahead), jnp.where(after, ahead, behind))
        return at

    each("wait_recv", ("pack", "visc", "edge"))
    sight = frame(1)
    for z in range(half):
        both = sight(REACH * z)
        vx[z, :, cols:] = both
        vx[z + half, :, cols:] = near(both, 2, 0)
    known = frame(2)

    def strip_field(j, place):
        return jnp.concatenate([ef[j], known(place)], axis=1)

    e, f = factor(vx, upx, downx, bed_drag * strip_field(0, 6 * REACH))
    b, t = (0.25 * offset_weight) / f, strip_field(1, 7 * REACH) / e
    for z in range(levels):
        k = levels - 1 - z
        put(bx, z, b)
        put(gx, z, vx[z] * b)
        put(tx, k, t)
        put(hx, k, vx[k] * t)
        if z < levels - 1:
            t = t * upx[k - 1]
            b = b * downx[z]

    main, halo = range(cols // 128), range(cols // 128, cols // 128 + 1)

    def strip(ref, row, tiles, first=0):
        return jnp.concatenate([ref[c, pl.ds(first * rows + row, levels, stride=rows), :] for c in tiles], axis=1)

    def own_row(row):
        return [strip(bot, row, main), strip(gbot, row, main), strip(gtop, row, main, 1), strip(top, row, main, 1)]

    def far_row(row):
        return [strip(ref, row, main) for ref in (bx, gx, hx, tx)]

    def side_row(row):
        return [strip(ref, row, halo) for ref in (bx, gx, hx, tx)]

    def corner_row(row):
        return [roll(val, 64, 1) for val in side_row(row)]

    def level_weights(mid):
        index = lax.broadcasted_iota(jnp.int32, mid.shape, 0)
        out = jnp.where(index == 0, 0.0, near(mid, -1, 0)) + jnp.where(index == levels - 1, 0.0, near(mid, 1, 0))
        return weigh(mid, out)

    def across(here, there):
        by_b, by_g = level_weights(here[2]), level_weights(here[3])
        width = here[0].shape[1]
        at = lax.broadcasted_iota(jnp.int32, (1, width), 1)
        parts = []
        for dy in (-1, 0, 1):
            which = 1 if dy != 0 else 0
            part = jnp.sum(by_b[which] * near(there[0], dy, 1) + by_g[which] * near(there[1], dy, 1), axis=0, keepdims=True)
            parts.append(part if dy == 0 else jnp.where(at == (0 if dy < 0 else width - 1), 0.0, part))
        return parts

    def join(first, second):
        return [jnp.concatenate(pair, axis=1) for pair in zip(first, second)]

    last = rows - 1
    lines = {}
    pieces = ((own_row(last), far_row(0)), (side_row(last), corner_row(0)))
    lines[2 * rows - 1] = join(*[across(low, high) for low, high in pieces])
    lines[2 * rows] = join(*[across(high, low) for low, high in pieces])
    pieces = ((far_row(last), own_row(0)), (corner_row(last), side_row(0)))
    lines[rows - 1] = join(*[across(low, high) for low, high in pieces])
    lines[rows] = join(*[across(high, low) for low, high in pieces])

    each("wait_recv", ("side",))
    tall_lane = lax.broadcasted_iota(jnp.int32, (3 * rows, 128), 1)

    def column(mine_side, dy):
        if dy == 0:
            tiles = [px_recv[0, mine_side], pk_send[mine_side, 0], px_recv[1, mine_side]]
        else:
            tiles = [pk_recv[DIRS.index((dx, dy)) - 2, 0] for dx in (-1, 0, 1)]
        return jnp.concatenate(tiles, axis=0)

    level_of = lax.rem(tall_lane, levels)

    def beside(here, there):
        out = jnp.where(level_of == 0, 0.0, near(here, -1, 1)) + jnp.where(level_of == levels - 1, 0.0, near(here, 1, 1))
        straight, slant = [jnp.where(tall_lane < 2 * levels, near(w, 2 * levels, 1), 0.0) for w in weigh(here, out)]
        return [jnp.sum((straight if dx == 0 else slant) * near(there, dx, 0), axis=1, keepdims=True) for dx in (-1, 0, 1)]

    west, east = (column(1, -1), column(0, 0)), (column(1, 0), column(0, 1))
    posts = {
        1: ((cols + 127, beside(west[0], west[1])), (cols - 1, beside(east[0], east[1]))),
        -1: ((0, beside(west[1], west[0])), (cols, beside(east[1], east[0]))),
    }

    def extend(j, mine, recv, packs, place):
        for tile, dx in enumerate((-1, 0, 1)):
            here = mine if dx == 0 else recv(0 if dx < 0 else 1)
            from_right, from_left = packs(dx, 1), packs(dx, -1)
            side = jnp.where(lane < REACH, roll(from_right, -place, 1), 0.0)
            side = jnp.where(lane >= 128 - REACH, roll(from_left, 128 - REACH - place, 1), side)
            ext[j, tile * rows:(tile + 1) * rows, :cols] = here
            ext[j, tile * rows:(tile + 1) * rows, cols:] = side

    def early(dx, dy):
        return pk_recv[DIRS.index((dx, dy)) - 2, 2]

    def late(dx, dy):
        return q_recv[DIRS.index((dx, dy)) - 2]

    each("wait_recv", ("wide", "less"))
    for j in range(3):
        extend(j, a_send[j], lambda i: a_recv[i, j], early, REACH * j)
    for j in range(2):
        extend(3 + j, c_send[j], lambda i: c_recv[i, j], early, REACH * (3 + j))
    each("wait_recv", ("late", "coef"))
    extend(5, k_send[0], lambda i: k_recv[i, 0], early, REACH * 5)
    wide_col = lax.broadcasted_iota(jnp.int32, (3 * rows, cols + 128), 1)
    for d, (dx, dy) in enumerate(DIRS):
        extend(BASE + d, k_send[1 + d], lambda i: k_recv[i, 1 + d], late, REACH * d)
        if dy != 0:
            whole = ext[BASE + d]
            for spot, parts in posts[dy]:
                whole = whole + jnp.where(wide_col == spot, parts[dx + 1], 0.0)
            ext[BASE + d] = whole
        if dx != 0:
            for row in ((rows - 1, 2 * rows - 1) if dx > 0 else (rows, 2 * rows)):
                ext[BASE + d, row:row + 1, :] = ext[BASE + d, row:row + 1, :] + lines[row][dy + 1]

    def coef(dx, dy):
        return ext[BASE + DIRS.index((dx, dy))]

    shares = (1.0 + cross_share, 1.0 - cross_share)

    def forth(q):
        surface = []
        for c in range(2):
            spread = ext[c] * q
            total = ext[5] * spread
            sums = {1: None, -1: None}
            for dy in (-1, 0, 1):
                turned = near(spread, dy, 1)
                for dx in (-1, 0, 1):
                    if (dx, dy) == (0, 0):
                        continue
                    val = coef(dx, dy) * near(turned, dx, 0)
                    if dx * dy == 0:
                        total = total + val
                    else:
                        sums[dx * dy] = val if sums[dx * dy] is None else sums[dx * dy] + val
            surface.append(total + shares[c] * sums[1] + shares[1 - c] * sums[-1])
        return surface

    def back(q, surface):
        result = regularize(q)
        for c in range(2):
            pull = surface[c]
            scaled = {0: pull, 1: shares[c] * pull, -1: shares[1 - c] * pull}
            basal = ext[5] * pull
            for dy in (-1, 0, 1):
                part = None
                for dx in (-1, 0, 1):
                    if (dx, dy) == (0, 0):
                        continue
                    val = near(coef(-dx, -dy) * scaled[dx * dy], dx, 0)
                    part = val if part is None else part + val
                basal = basal + near(part, dy, 1)
            result = result + ext[c] * basal
        return result

    def regularize(q):
        around = near(q, 1, 0) + near(q, -1, 0) + near(q, 1, 1) + near(q, -1, 1)
        return reg_gamma * (q + reg_smooth * (4.0 * q - around))

    def hessian(q):
        return back(q, forth(q))

    def mine(x):
        return x[rows:2 * rows, :cols]

    image = hessian(ext[2])
    r0 = ext[4] - image
    p0 = ext[3] * r0
    w0 = hessian(p0)
    y0 = ext[3] * w0
    surface = forth(y0)
    curve0 = mine(surface[0]) * mine(surface[0]) + mine(surface[1]) * mine(surface[1]) + mine(y0 * regularize(y0))
    full_y0 = y0
    r0, p0, w0, y0 = mine(r0), mine(p0), mine(w0), mine(y0)

    def total(x):
        return jnp.sum(jnp.sum(x, axis=0, keepdims=True), axis=1, keepdims=True)

    one_lane = lax.broadcasted_iota(jnp.int32, (1, 128), 1)
    sums = jnp.zeros((1, 128), jnp.float32)
    for j, val in enumerate((r0 * p0, p0 * w0, w0 * y0, curve0)):
        sums = jnp.where(one_lane == j, total(val), sums)
    red[...] = sums

    def to_peer(peer):
        return pltpu.make_async_remote_copy(
            src_ref=red, dst_ref=slots.at[me], send_sem=r_send, recv_sem=r_recv,
            device_id=peer, device_id_type=LOGICAL,
        )

    everybody = pltpu.make_async_remote_copy(
        src_ref=slots.at[pl.ds(0, n - 1)], dst_ref=slots.at[pl.ds(0, n - 1)], send_sem=r_send, recv_sem=r_recv,
        device_id=me, device_id_type=LOGICAL,
    )

    def send(j, c):
        peer = lax.rem(2 * n - 1 - me + j, n)

        @pl.when(peer != me)
        def _():
            to_peer(peer).start()
        return c

    pl.semaphore_wait(all_in, ny - 1)
    lax.fori_loop(0, n, send, 0, unroll=8)
    u0 = mine(back(full_y0, surface))
    each("wait_send", [name for name, _ in kinds])
    everybody.wait_recv()
    slots[me] = sums
    everyone = jnp.sum(slots[...], axis=0)

    def value(j):
        return jnp.sum(jnp.where(one_lane == j, everyone, 0.0), axis=1, keepdims=True)

    rz0, pw, wy, yu = value(0), value(1), value(2), value(3)
    a0 = rz0 / pw
    rz1 = a0 * a0 * wy - rz0
    beta = rz1 / rz0
    more = 1.0 + beta
    curve = more * (more * pw - 2.0 * a0 * wy) + a0 * a0 * yu
    a1 = rz1 / curve
    out_ref[0] = warm_ref[...] + (a0 * p0 + a1 * (more * p0 - a0 * y0))
    out_ref[1] = grad_ref[...] + (-mine(image) - a0 * w0 - a1 * (more * w0 - a0 * u0))
    everybody.wait_send()


def solution(mesh):
    nx, ny = mesh.shape["gx"], mesh.shape["gy"]
    n = nx * ny

    def on_device(gradient, warm_start, viscosity, friction_coef, slide_dir, obs_weight, ice_mask, grounded):
        levels, rows, cols = viscosity.shape
        vmem = pl.BlockSpec(memory_space=pltpu.VMEM)
        f32 = lambda *shape: pltpu.VMEM(shape, jnp.float32)
        flat = (gradient, warm_start, viscosity, friction_coef, slide_dir, obs_weight, ice_mask, grounded)
        out = pl.pallas_call(
            functools.partial(kernel, nx, ny),
            out_shape=f32(2, rows, cols),
            in_specs=[pl.BlockSpec(memory_space=pl.ANY)] * 8,
            out_specs=vmem,
            scratch_shapes=[
                *(pltpu.VMEM(a.shape, a.dtype) for a in flat),
                f32(levels, rows, cols), f32(levels, rows, cols),
                *(f32(cols // 128, levels * rows, 128) for _ in range(2)),
                *(f32(cols // 128, (levels + 2) * rows, 128) for _ in range(2)),
                *(f32(levels, rows, cols + 128) for _ in range(3)),
                *(f32(cols // 128 + 1, levels * rows, 128) for _ in range(4)),
                f32(2, rows, cols), f32(2, rows, cols),
                f32(3, rows, cols), f32(2, 3, rows, cols),
                f32(2, rows, cols), f32(2, 2, rows, cols),
                f32(9, rows, cols), f32(2, 9, rows, cols),
                f32(2, 3, rows, 128), f32(6, 3, rows, 128), f32(2, 2, rows, 128),
                f32(2, rows, 128), f32(6, rows, 128),
                f32(BASE + 8, 3 * rows, cols + 128),
                f32(1, 128), f32(n, 1, 128),
                pltpu.SemaphoreType.DMA((8,)),
                pltpu.SemaphoreType.DMA((24,)), pltpu.SemaphoreType.DMA((24,)),
                pltpu.SemaphoreType.DMA, pltpu.SemaphoreType.DMA,
                pltpu.SemaphoreType.REGULAR,
            ],
            compiler_params=pltpu.CompilerParams(collective_id=0, has_side_effects=True),
        )(*flat)
        return out[0], out[1]

    flat = P("gx", "gy")
    deep = P(None, "gx", "gy")
    return jax.shard_map(
        on_device,
        mesh=mesh,
        in_specs=(flat, flat, deep, flat, deep, flat, flat, flat),
        out_specs=(flat, flat),
        check_vma=False,
    )
```

time: 21.7 us -> 17.7 us (0.82)
  Pallas kernels: 20.3 us -> 16.3 us
    pallas_call x1, Pallas kernels: 20.3 us -> 16.3 us  [on_device(): pl.pallas_call(functools.partial(kernel, nx, ny), out_shape=f32(2, rows,...]
where the time goes in v2:
time: 17.7 us; the launch traced here: 17.5 us
  Pallas kernels  16.3 us (92%)
  between operations  0.64 us (4%)
  local copies, waits for them, and re-layouts  0.61 us (3%)
    pallas_call x1, Pallas kernels, on_device(): pl.pallas_call(functools.partial(kernel, nx, ny), out_shape=f32(2, rows,...  16.3 us
    squeeze x1, local copies, waits for them, and re-layouts, on_device(): return (out[0], out[1])  0.61 us

profile of v2, /device:TPU:0, one launch (start us, length us, event | category | flops | bytes accessed | tf_op | source)
XLA Modules:
  0.0 17.5 jit_solution(11303354790695455224)
XLA Ops:
  0.6 16.3 %shard_map.95 = f32[2,8,256]{2,1,0:T(8,128)S(1)} custom-call(f32[8,256]{1,0:T(8,128)} %grad_in.1, f32[8,256]{1,0:T(8,128)} %warm_in.1, f32[32,8,256]{2,1,0:T(8,128)} %visc_in.1, f32[8,256]{1,0:T(8,128)} %fric_in.1, f32[2,8,256]{2,1,0:T(8,128)} %slide_in.1, f32[8,256]{1,0:T(8,128)} %obs_in.1, s32[8,256]{1,0:T(8,128)} %ice_in.1, s32[8,256]{1,0:T(8,128)} %ground_in.1), custom_call_target="tpu_custom_call" | custom-call | tf_op jit(solution)/shard_map/pallas_call | solution.py:554
  16.9 0.6 %slice_bitcast_fusion = (f32[8,256]{1,0:T(8,128)}, f32[8,256]{1,0:T(8,128)}) fusion(f32[2,8,256]{2,1,0:T(8,128)S(1)} %shard_map.95), kind=kLoop, calls=%fused_computation | loop fusion | bytes 32768 | tf_op jit(solution)/shard_map/squeeze | solution.py:581

commit v3 on v2

--- a/solution.py
+++ b/solution.py
@@ -45,9 +45,9 @@
     up, down, bot, gbot, top, gtop,
     vx, upx, downx, bx, gx, tx, hx,
     e_send, ef, a_send, a_recv, c_send, c_recv, k_send, k_recv,
-    pk_send, pk_recv, px_recv, q_send, q_recv,
+    q_send, q_recv, d_send, d_recv, px_send, px_recv,
     ext, red, slots,
-    load_sem, s_send, s_recv, r_send, r_recv, all_in,
+    load_sem, s_send, s_recv, r_send, r_recv, entered,
 ):
     levels, rows, cols = visc_ref.shape
     n = nx * ny
@@ -74,17 +74,28 @@
 
     for load in loads:
         load.start()
-    expected = nx - 1 + ny - 1
-    for d in range(4, 8):
+    expected = ny - 1
+    for d in (0, 1):
         expected = expected + exists(d).astype(jnp.int32)
 
         @pl.when(exists(d))
         def _():
-            greet(ix + DIRS[d][0], iy + DIRS[d][1])
-    for k in range(1, nx):
-        greet(lax.rem(ix + k, nx), iy)
+            greet(ix + DIRS[d][0], iy)
     for k in range(1, ny):
         greet(ix, lax.rem(iy + k, ny))
+    rounds = entered.shape[0]
+
+    def herald(r):
+        for side, step in ((1, -(2 ** r)), (0, 2 ** r)):
+            @pl.when((ix + step >= 0) & (ix + step < nx))
+            def _():
+                pl.semaphore_signal(entered.at[r, side], inc=1, device_id=(ix + step, iy), device_id_type=MESH)
+
+    def hear(r):
+        for side, step in ((0, -(2 ** r)), (1, 2 ** r)):
+            @pl.when((ix + step >= 0) & (ix + step < nx))
+            def _():
+                pl.semaphore_wait(entered.at[r, side], 1)
 
     def copy(src, dst, d, sem):
         dx, dy = DIRS[d]
@@ -104,26 +115,21 @@
             return pl.ds(0 if dx < 0 else rows - k, k)
 
         return {
-            "pack": lambda: copy(pk_send.at[side], pk_recv.at[o - 2], d, 0),
-            "visc": lambda: copy(visc_ref.at[:, part(1), :], vx.at[:, part(1), pl.ds(0, cols)], d, 0),
-            "late": lambda: copy(q_send.at[side], q_recv.at[o - 2], d, 8),
+            "visc": lambda: copy(visc_ref.at[:, part(1), :], vx.at[:, part(1), :], d, 0),
+            "slant": lambda: copy(d_send.at[d - 4], d_recv.at[o - 4], d, 0),
             "edge": lambda: copy(e_send.at[:, part(1), :], ef.at[:, part(1), :], d, 8),
-            "side": lambda: copy(pk_send.at[:, 0], px_recv.at[o], d, 16),
-            "wide": lambda: copy(a_send.at[:, part(REACH), :], a_recv.at[o, :, part(REACH), :], d, 18),
-            "less": lambda: copy(c_send.at[:, part(REACH - 2), :], c_recv.at[o, :, part(REACH - 2), :], d, 20),
-            "coef": lambda: copy(k_send.at[:, part(REACH - 1), :], k_recv.at[o, :, part(REACH - 1), :], d, 22),
+            "late": lambda: copy(q_send.at[side], q_recv.at[o - 2], d, 0),
+            "side": lambda: copy(px_send.at[:, part(REACH), :], px_recv.at[o, :, part(REACH), :], d, 10),
+            "wide": lambda: copy(a_send.at[:, part(REACH), :], a_recv.at[o, :, part(REACH), :], d, 12),
+            "less": lambda: copy(c_send.at[:, part(REACH - 2), :], c_recv.at[o, :, part(REACH - 2), :], d, 14),
+            "coef": lambda: copy(k_send.at[:, part(REACH - 1), :], k_recv.at[o, :, part(REACH - 1), :], d, 16),
         }[what]()
 
-    beside_x, others = (0, 1), range(2, 8)
-    kinds = (
-        ("pack", others), ("visc", beside_x), ("edge", beside_x), ("side", beside_x), ("wide", beside_x), ("less", beside_x),
-        ("late", others), ("coef", beside_x),
-    )
-
-    def each(action, names):
-        for name, towards in kinds:
-            if name not in names:
-                continue
+    along_x, along_y, aslant = (0, 1), (2, 3), (4, 5, 6, 7)
+    for_x, for_y = ("visc", "edge", "wide", "less", "side", "coef"), ("late",)
+
+    def each(action, names, towards):
+        for name in names:
             for d in towards:
                 @pl.when(exists(d))
                 def _():
@@ -142,15 +148,14 @@
         def _():
             if d < 2:
                 row = pl.ds(rows - 1 if d == 0 else 0, 1)
-                fill(vx.at[:, row, pl.ds(0, cols)], 1.0)
+                fill(vx.at[:, row, :], 1.0)
                 fill(ef.at[:, row, :])
                 for ref in (px_recv, a_recv, c_recv, k_recv):
                     fill(ref.at[d])
+            elif d < 4:
+                fill(q_recv.at[d - 2])
             else:
-                fill(pk_recv.at[d - 2, 0])
-                fill(pk_recv.at[d - 2, 1], 1.0)
-                fill(pk_recv.at[d - 2, 2])
-                fill(q_recv.at[d - 2])
+                fill(d_recv.at[d - 4])
 
     for load in loads:
         load.wait()
@@ -199,16 +204,38 @@
     def get(ref, z):
         return jnp.concatenate([ref[c, layer(z), :] for c in range(ref.shape[0])], axis=1)
 
-    e, f = factor(visc_ref, up, down, bed_drag * friction)
     zero = jnp.zeros((rows, cols), jnp.float32)
     for ref in (top, gtop):
         put(ref, 0, zero)
         put(ref, levels + 1, zero)
 
     blank = jnp.zeros((rows, 128), jnp.float32)
-    half = levels // 2
+    def rim(val):
+        return jnp.where(lane < 64, val[:, :128], val[:, cols - 128:])
+
+    def within(place, width):
+        start = place % 128
+        return (lane >= start) & (lane < start + width)
+
+    def pack(fields, place, left, right):
+        for val in fields:
+            moved = roll(rim(val), place, 1)
+            left = jnp.where(within(place, REACH), moved, left)
+            right = jnp.where(within(place - REACH, REACH), moved, right)
+            place += REACH
+        return left, right
+
+    for j, val in enumerate((sum_src, dif_src, warm_ref[...])):
+        a_send[j] = val
+    for j, val in enumerate((inverse, grad_ref[...])):
+        c_send[j] = val
+    for j, val in enumerate((friction, watch)):
+        e_send[j] = val
+    e, f = factor(visc_ref, up, down, bed_drag * friction)
+    pl.semaphore_wait(barrier, expected)
+    herald(0)
+    each("start", ("visc", "edge", "wide", "less"), along_x)
     left, right = blank, blank
-    near_left, near_right = [blank + 1.0] * 2, [blank + 1.0] * 2
     b, t = (0.25 * offset_weight) / f, watch / e
     for z in range(levels):
         k = levels - 1 - z
@@ -219,43 +246,39 @@
         put(top, k + 1, t)
         put(gtop, k + 1, h)
         for place, val in ((z, b), (levels + z, g), (2 * levels + k, h), (3 * levels + k, t)):
-            left = jnp.where(lane == place, roll(val[:, :128], place, 1), left)
-            right = jnp.where(lane == place, roll(val[:, cols - 128:], place + 1, 1), right)
-        place = REACH * (z % half)
-        here = (lane >= place) & (lane < place + REACH)
-        near_left[z // half] = jnp.where(here, roll(v[:, :128], place, 1), near_left[z // half])
-        near_right[z // half] = jnp.where(here, roll(v[:, cols - 128:], place + REACH, 1), near_right[z // half])
+            moved = roll(rim(val), place, 1)
+            left = jnp.where(lane == place, moved, left)
+            right = jnp.where(lane == (place - 1) % 128, moved, right)
         if z < levels - 1:
             t = t * up[k - 1]
             b = b * down[z]
     through = t
-
-    def pack(fields, place, left, right):
-        for val in fields:
-            here = (lane >= place) & (lane < place + REACH)
-            left = jnp.where(here, roll(val[:, :128], place, 1), left)
-            right = jnp.where(here, roll(val[:, cols - 128:], place - (128 - REACH), 1), right)
-            place += REACH
-        return left, right
-
-    for j, val in enumerate((sum_src, dif_src, warm_ref[...])):
-        a_send[j] = val
-    for j, val in enumerate((inverse, grad_ref[...])):
-        c_send[j] = val
+    right = roll(right, 1, 1)
     k_send[0] = through
-    for j, val in enumerate((friction, watch)):
-        e_send[j] = val
-    fields = pack((sum_src, dif_src, warm_ref[...], inverse, grad_ref[...], through, friction, watch), 0, blank, blank)
-    folded = (prow == 1) | (prow == 2)
-    for side, strip, sight in ((0, left, near_left), (1, right, near_right)):
-        pk_send[side, 0] = strip
-        pk_send[side, 1] = jnp.where(folded, roll(sight[1], 2, 0), sight[0])
-        pk_send[side, 2] = fields[side]
-
-    pl.semaphore_wait(barrier, expected)
-    each("start", ("pack", "visc", "edge", "side", "wide", "less"))
-    for k in range(1, ny):
-        pl.semaphore_signal(all_in, inc=1, device_id=(ix, lax.rem(iy + k, ny)), device_id_type=MESH)
+    px_send[0], px_send[1] = left, right
+    each("start", ("side",), along_x)
+    spans = [(q, tile) for q in range(4) for tile in range(levels // rows)]
+
+    def spot(q, tile):
+        return tile * (128 * rows // levels) + REACH * q
+
+    for side in (0, 1):
+        q_send[side, 1] = (left, right)[side]
+        d_send[side, 1] = (left, right)[side]
+        d_send[2 + side, 1] = (left, right)[side]
+    for j, row in enumerate((0, rows - 1)):
+        corner = [blank, blank]
+        for q, tile in spans:
+            ref, first = ((bot, 0), (gbot, 0), (gtop, 1), (top, 1))[q]
+            span = pl.ds((first + tile * rows) * rows + row, rows, stride=rows)
+            place = spot(q, tile)
+            moved = roll(jnp.where(lane < 64, ref[0, span, :], ref[cols // 128 - 1, span, :]), place, 1)
+            corner[0] = jnp.where(within(place, REACH), moved, corner[0])
+            corner[1] = jnp.where(within(place - REACH, REACH), moved, corner[1])
+        for side in (0, 1):
+            q_send[side, 2 + j] = corner[side]
+            d_send[2 * j + side, 2] = corner[side]
+    fields = pack((sum_src, dif_src, warm_ref[...], inverse, grad_ref[...], through), 0, blank, blank)
 
     def weigh(mid, out):
         return 2.0 * mid + out, mid + (2.0 / 3.0) * out
@@ -275,152 +298,174 @@
 
     row_id = lax.broadcasted_iota(jnp.int32, (rows, cols), 0)
     col_id = lax.broadcasted_iota(jnp.int32, (rows, cols), 1)
-    coefs = list(lax.fori_loop(0, levels, gather, (zero,) * 8, unroll=8))
+    coefs = list(lax.fori_loop(0, levels, gather, (zero,) * 8, unroll=16))
     for d, (dx, dy) in enumerate(DIRS):
         if dx != 0:
             coefs[d] = jnp.where(row_id == (0 if dx < 0 else rows - 1), 0.0, near(coefs[d], dx, 0))
         if dy != 0:
             coefs[d] = jnp.where(col_id == (0 if dy < 0 else cols - 1), 0.0, coefs[d])
         k_send[1 + d] = coefs[d]
-    q_send[0], q_send[1] = pack(coefs, 0, blank, blank)
-    each("start", ("late", "coef"))
-
-    def pick(packs, dx, dy):
-        return packs[DIRS.index((dx, dy)) - 2]
-
-    def corner(which, dy):
-        flat = [pk_recv[DIRS.index((dx, dy)) - 2, which] for dx in (-1, 1)]
-        return jnp.where((prow == 0) | (prow == 2), flat[1], flat[0])
-
-    inner = (lane >= 32) & (lane < 96)
-    after = lane < 64
-
-    def frame(which):
-        sides = [pk_recv[DIRS.index((0, dy)) - 2, which] for dy in (1, -1)]
-        corners = [corner(which, dy) for dy in (1, -1)]
-
-        def at(place):
-            ahead = jnp.where(inner, roll(corners[0], 64 - place, 1), roll(sides[0], -place, 1))
-            behind = jnp.where(inner, roll(corners[1], 64 - REACH - place, 1), roll(sides[1], -REACH - place, 1))
-            return jnp.where(inner, jnp.where(lane < 64, behind, ahead), jnp.where(after, ahead, behind))
-        return at
-
-    each("wait_recv", ("pack", "visc", "edge"))
-    sight = frame(1)
-    for z in range(half):
-        both = sight(REACH * z)
-        vx[z, :, cols:] = both
-        vx[z + half, :, cols:] = near(both, 2, 0)
-    known = frame(2)
-
-    def strip_field(j, place):
-        return jnp.concatenate([ef[j], known(place)], axis=1)
-
-    e, f = factor(vx, upx, downx, bed_drag * strip_field(0, 6 * REACH))
-    b, t = (0.25 * offset_weight) / f, strip_field(1, 7 * REACH) / e
-    for z in range(levels):
-        k = levels - 1 - z
-        put(bx, z, b)
-        put(gx, z, vx[z] * b)
-        put(tx, k, t)
-        put(hx, k, vx[k] * t)
-        if z < levels - 1:
-            t = t * upx[k - 1]
-            b = b * downx[z]
-
-    main, halo = range(cols // 128), range(cols // 128, cols // 128 + 1)
-
-    def strip(ref, row, tiles, first=0):
-        return jnp.concatenate([ref[c, pl.ds(first * rows + row, levels, stride=rows), :] for c in tiles], axis=1)
+    fields = pack(coefs, REACH * BASE, *fields)
+    for side in (0, 1):
+        q_send[side, 0] = fields[side]
+        for j in (0, 1):
+            d_send[2 * j + side, 0] = fields[side]
+    each("start", ("late",), along_y)
+    hear(0)
+    each("start", ("slant",), aslant)
+    each("start", ("coef",), along_x)
+    if rounds > 1:
+        herald(1)
+
+    def respond(v, up, down, drag, sight, refs):
+        e, f = factor(v, up, down, drag)
+        b, t = (0.25 * offset_weight) / f, sight / e
+        for z in range(levels):
+            k = levels - 1 - z
+            put(refs[0], z, b)
+            put(refs[1], z, v[z] * b)
+            put(refs[2], k, v[k] * t)
+            put(refs[3], k, t)
+            if z < levels - 1:
+                t = t * up[k - 1]
+                b = b * down[z]
+
+    far = (bx, gx, hx, tx)
+    def strip(ref, row, first=0):
+        return jnp.concatenate(
+            [ref[c, pl.ds(first * rows + row, levels, stride=rows), :] for c in range(ref.shape[0])], axis=1
+        )
 
     def own_row(row):
-        return [strip(bot, row, main), strip(gbot, row, main), strip(gtop, row, main, 1), strip(top, row, main, 1)]
+        return [strip(bot, row), strip(gbot, row), strip(gtop, row, 1), strip(top, row, 1)]
 
     def far_row(row):
-        return [strip(ref, row, main) for ref in (bx, gx, hx, tx)]
+        return [strip(ref, row) for ref in far]
+
+    phase = lax.rem(lane, 128 * rows // levels)
+
+    def unfold(ahead, behind):
+        mixed = []
+        for odd in (0, REACH):
+            first = (phase >= odd) & (phase < odd + REACH) | (phase >= odd + 2 * REACH) & (phase < odd + 3 * REACH)
+            mixed.append(jnp.where(first, ahead, behind))
+        return [
+            jnp.concatenate([roll(mixed[q % 2], -spot(q, tile), 1) for tile in range(levels // rows)], axis=0)
+            for q in range(4)
+        ]
 
     def side_row(row):
-        return [strip(ref, row, halo) for ref in (bx, gx, hx, tx)]
+        return unfold(*[q_recv[y, 2 if row == 0 else 3] for y in (1, 0)])
 
     def corner_row(row):
-        return [roll(val, 64, 1) for val in side_row(row)]
+        dx = 1 if row == 0 else -1
+        return unfold(*[d_recv[DIRS.index((dx, dy)) - 4, 2] for dy in (1, -1)])
 
     def level_weights(mid):
         index = lax.broadcasted_iota(jnp.int32, mid.shape, 0)
         out = jnp.where(index == 0, 0.0, near(mid, -1, 0)) + jnp.where(index == levels - 1, 0.0, near(mid, 1, 0))
         return weigh(mid, out)
 
+    def ready(vals):
+        moved = [[near(val, dy, 1) for val in vals[:2]] for dy in (-1, 0, 1)]
+        return level_weights(vals[2]), level_weights(vals[3]), moved
+
     def across(here, there):
-        by_b, by_g = level_weights(here[2]), level_weights(here[3])
-        width = here[0].shape[1]
+        width = there[2][0][0].shape[1]
         at = lax.broadcasted_iota(jnp.int32, (1, width), 1)
         parts = []
         for dy in (-1, 0, 1):
             which = 1 if dy != 0 else 0
-            part = jnp.sum(by_b[which] * near(there[0], dy, 1) + by_g[which] * near(there[1], dy, 1), axis=0, keepdims=True)
+            by_b, by_g = there[2][dy + 1]
+            part = jnp.sum(here[0][which] * by_b + here[1][which] * by_g, axis=0, keepdims=True)
             parts.append(part if dy == 0 else jnp.where(at == (0 if dy < 0 else width - 1), 0.0, part))
         return parts
 
-    def join(first, second):
-        return [jnp.concatenate(pair, axis=1) for pair in zip(first, second)]
-
     last = rows - 1
-    lines = {}
-    pieces = ((own_row(last), far_row(0)), (side_row(last), corner_row(0)))
-    lines[2 * rows - 1] = join(*[across(low, high) for low, high in pieces])
-    lines[2 * rows] = join(*[across(high, low) for low, high in pieces])
-    pieces = ((far_row(last), own_row(0)), (corner_row(last), side_row(0)))
-    lines[rows - 1] = join(*[across(low, high) for low, high in pieces])
-    lines[rows] = join(*[across(high, low) for low, high in pieces])
-
-    each("wait_recv", ("side",))
-    tall_lane = lax.broadcasted_iota(jnp.int32, (3 * rows, 128), 1)
-
-    def column(mine_side, dy):
-        if dy == 0:
-            tiles = [px_recv[0, mine_side], pk_send[mine_side, 0], px_recv[1, mine_side]]
-        else:
-            tiles = [pk_recv[DIRS.index((dx, dy)) - 2, 0] for dx in (-1, 0, 1)]
+    low, high = ready(own_row(0)), ready(own_row(last))
+    each("wait_recv", ("visc", "edge"), along_x)
+    respond(vx, upx, downx, bed_drag * ef[0], ef[1], far)
+    below, above = ready(far_row(last)), ready(far_row(0))
+    lines = {
+        2 * rows - 1: across(high, above), 2 * rows: across(above, high),
+        rows - 1: across(below, low), rows: across(low, below),
+    }
+    each("wait_recv", ("side", "wide", "less"), along_x)
+    each("wait_recv", ("late",), along_y)
+    low, high = ready(side_row(0)), ready(side_row(last))
+    level_of = lax.rem(lane, levels)
+
+    def beyond(dx, dy, which):
+        return q_recv[0 if dy < 0 else 1, which] if dx == 0 else d_recv[DIRS.index((dx, dy)) - 4, which]
+
+    def column(mine_side):
+        return [px_recv[0, mine_side], q_send[mine_side, 1], px_recv[1, mine_side]]
+
+    def slope(here):
+        out = jnp.where(level_of == 0, 0.0, near(here, -1, 1)) + jnp.where(level_of == levels - 1, 0.0, near(here, 1, 1))
+        return [jnp.where(lane < 2 * levels, near(w, 2 * levels, 1), 0.0) for w in weigh(here, out)]
+
+    def stack(tiles):
         return jnp.concatenate(tiles, axis=0)
 
-    level_of = lax.rem(tall_lane, levels)
-
-    def beside(here, there):
-        out = jnp.where(level_of == 0, 0.0, near(here, -1, 1)) + jnp.where(level_of == levels - 1, 0.0, near(here, 1, 1))
-        straight, slant = [jnp.where(tall_lane < 2 * levels, near(w, 2 * levels, 1), 0.0) for w in weigh(here, out)]
+    def beside(slopes, there):
+        straight, slant = [stack([each_slope[i] for each_slope in slopes]) for i in (0, 1)]
+        there = stack(there)
         return [jnp.sum((straight if dx == 0 else slant) * near(there, dx, 0), axis=1, keepdims=True) for dx in (-1, 0, 1)]
 
-    west, east = (column(1, -1), column(0, 0)), (column(1, 0), column(0, 1))
-    posts = {
-        1: ((cols + 127, beside(west[0], west[1])), (cols - 1, beside(east[0], east[1]))),
-        -1: ((0, beside(west[1], west[0])), (cols, beside(east[1], east[0]))),
+    inside = [[slope(tile) for tile in column(side)] for side in (0, 1)]
+    outside = [slope(beyond(0, dy, 1)) for dy in (-1, 1)]
+
+    even = within(0, REACH)
+    for j in range(2, BASE + 8, 2):
+        even = even | within(REACH * j, REACH)
+    odd = within(REACH, REACH)
+    for j in range(3, BASE + 8, 2):
+        odd = odd | within(REACH * j, REACH)
+
+    def mix(dx):
+        return [jnp.where(first, beyond(dx, 1, 0), beyond(dx, -1, 0)) for first in (even, odd)]
+
+    def extend(j, mine, recv):
+        for tile, here in enumerate((recv(0), mine, recv(1))):
+            ext[j, tile * rows:(tile + 1) * rows, :cols] = here
+
+    kept = (lane < REACH) | (lane >= 128 - REACH)
+
+    def frame(j, tile, mixed):
+        ext[j, tile * rows:(tile + 1) * rows, cols:] = jnp.where(kept, roll(mixed[j % 2], -REACH * j, 1), 0.0)
+
+    mixed = mix(0)
+    for j in range(3):
+        extend(j, a_send[j], lambda i: a_recv[i, j])
+    for j in range(2):
+        extend(3 + j, c_send[j], lambda i: c_recv[i, j])
+    for j in range(BASE + 8):
+        frame(j, 1, mixed)
+
+    each("wait_recv", ("slant",), aslant)
+    below, above = ready(corner_row(last)), ready(corner_row(0))
+    edges = {
+        2 * rows - 1: across(high, above), 2 * rows: across(above, high),
+        rows - 1: across(below, low), rows: across(low, below),
     }
-
-    def extend(j, mine, recv, packs, place):
-        for tile, dx in enumerate((-1, 0, 1)):
-            here = mine if dx == 0 else recv(0 if dx < 0 else 1)
-            from_right, from_left = packs(dx, 1), packs(dx, -1)
-            side = jnp.where(lane < REACH, roll(from_right, -place, 1), 0.0)
-            side = jnp.where(lane >= 128 - REACH, roll(from_left, 128 - REACH - place, 1), side)
-            ext[j, tile * rows:(tile + 1) * rows, :cols] = here
-            ext[j, tile * rows:(tile + 1) * rows, cols:] = side
-
-    def early(dx, dy):
-        return pk_recv[DIRS.index((dx, dy)) - 2, 2]
-
-    def late(dx, dy):
-        return q_recv[DIRS.index((dx, dy)) - 2]
-
-    each("wait_recv", ("wide", "less"))
-    for j in range(3):
-        extend(j, a_send[j], lambda i: a_recv[i, j], early, REACH * j)
-    for j in range(2):
-        extend(3 + j, c_send[j], lambda i: c_recv[i, j], early, REACH * (3 + j))
-    each("wait_recv", ("late", "coef"))
-    extend(5, k_send[0], lambda i: k_recv[i, 0], early, REACH * 5)
+    for row in lines:
+        lines[row] = [jnp.concatenate(pair, axis=1) for pair in zip(lines[row], edges[row])]
+    posts = {1: [], -1: []}
+    for side, dy in ((0, -1), (1, 1)):
+        tiles = [beyond(dx, dy, 1) for dx in (-1, 0, 1)]
+        slopes = [slope(tiles[0]), outside[side], slope(tiles[2])]
+        posts[dy].append((cols - 1 if dy > 0 else 0, beside(inside[side], tiles)))
+        posts[-dy].append((cols if dy > 0 else cols + 127, beside(slopes, column(side))))
+    for tile, dx in ((0, -1), (2, 1)):
+        mixed = mix(dx)
+        for j in range(BASE + 8):
+            frame(j, tile, mixed)
+    each("wait_recv", ("coef",), along_x)
+    extend(5, k_send[0], lambda i: k_recv[i, 0])
     wide_col = lax.broadcasted_iota(jnp.int32, (3 * rows, cols + 128), 1)
     for d, (dx, dy) in enumerate(DIRS):
-        extend(BASE + d, k_send[1 + d], lambda i: k_recv[i, 1 + d], late, REACH * d)
+        extend(BASE + d, k_send[1 + d], lambda i: k_recv[i, 1 + d])
         if dy != 0:
             whole = ext[BASE + d]
             for spot, parts in posts[dy]:
@@ -519,10 +564,15 @@
             to_peer(peer).start()
         return c
 
-    pl.semaphore_wait(all_in, ny - 1)
+    for r in range(1, rounds):
+        hear(r)
+        if r + 1 < rounds:
+            herald(r + 1)
     lax.fori_loop(0, n, send, 0, unroll=8)
     u0 = mine(back(full_y0, surface))
-    each("wait_send", [name for name, _ in kinds])
+    each("wait_send", for_x, along_x)
+    each("wait_send", for_y, along_y)
+    each("wait_send", ("slant",), aslant)
     everybody.wait_recv()
     slots[me] = sums
     everyone = jnp.sum(slots[...], axis=0)
@@ -561,20 +611,20 @@
                 f32(levels, rows, cols), f32(levels, rows, cols),
                 *(f32(cols // 128, levels * rows, 128) for _ in range(2)),
                 *(f32(cols // 128, (levels + 2) * rows, 128) for _ in range(2)),
-                *(f32(levels, rows, cols + 128) for _ in range(3)),
-                *(f32(cols // 128 + 1, levels * rows, 128) for _ in range(4)),
+                *(f32(levels, rows, cols) for _ in range(3)),
+                *(f32(cols // 128, levels * rows, 128) for _ in range(4)),
                 f32(2, rows, cols), f32(2, rows, cols),
                 f32(3, rows, cols), f32(2, 3, rows, cols),
                 f32(2, rows, cols), f32(2, 2, rows, cols),
                 f32(9, rows, cols), f32(2, 9, rows, cols),
-                f32(2, 3, rows, 128), f32(6, 3, rows, 128), f32(2, 2, rows, 128),
-                f32(2, rows, 128), f32(6, rows, 128),
+                f32(2, 4, rows, 128), f32(2, 4, rows, 128),
+                f32(4, 3, rows, 128), f32(4, 3, rows, 128), f32(2, rows, 128), f32(2, 2, rows, 128),
                 f32(BASE + 8, 3 * rows, cols + 128),
                 f32(1, 128), f32(n, 1, 128),
                 pltpu.SemaphoreType.DMA((8,)),
-                pltpu.SemaphoreType.DMA((24,)), pltpu.SemaphoreType.DMA((24,)),
+                pltpu.SemaphoreType.DMA((18,)), pltpu.SemaphoreType.DMA((18,)),
                 pltpu.SemaphoreType.DMA, pltpu.SemaphoreType.DMA,
-                pltpu.SemaphoreType.REGULAR,
+                pltpu.SemaphoreType.REGULAR((max(1, (nx - 1).bit_length()), 2)),
             ],
             compiler_params=pltpu.CompilerParams(collective_id=0, has_side_effects=True),
         )(*flat)

time: 17.7 us -> 17.1 us (0.966)
  Pallas kernels: 16.3 us -> 15.7 us
    pallas_call x1, Pallas kernels: 16.3 us -> 15.7 us  [on_device(): pl.pallas_call(functools.partial(kernel, nx, ny), out_shape=f32(2, rows,...]
where the time goes in v3:
time: 17.1 us; the launch traced here: 16.9 us
  Pallas kernels  15.7 us (92%)
  between operations  0.64 us (4%)
  local copies, waits for them, and re-layouts  0.61 us (4%)
    pallas_call x1, Pallas kernels, on_device(): pl.pallas_call(functools.partial(kernel, nx, ny), out_shape=f32(2, rows,...  15.7 us
    squeeze x1, local copies, waits for them, and re-layouts, on_device(): return (out[0], out[1])  0.61 us

profile of v3, /device:TPU:0, one launch (start us, length us, event | category | flops | bytes accessed | tf_op | source)
XLA Modules:
  0.0 16.9 jit_solution(4343582322853111797)
XLA Ops:
  0.6 15.7 %shard_map.95 = f32[2,8,256]{2,1,0:T(8,128)S(1)} custom-call(f32[8,256]{1,0:T(8,128)} %grad_in.1, f32[8,256]{1,0:T(8,128)} %warm_in.1, f32[32,8,256]{2,1,0:T(8,128)} %visc_in.1, f32[8,256]{1,0:T(8,128)} %fric_in.1, f32[2,8,256]{2,1,0:T(8,128)} %slide_in.1, f32[8,256]{1,0:T(8,128)} %obs_in.1, s32[8,256]{1,0:T(8,128)} %ice_in.1, s32[8,256]{1,0:T(8,128)} %ground_in.1), custom_call_target="tpu_custom_call" | custom-call | tf_op jit(solution)/shard_map/pallas_call | solution.py:604
  16.3 0.6 %slice_bitcast_fusion = (f32[8,256]{1,0:T(8,128)}, f32[8,256]{1,0:T(8,128)}) fusion(f32[2,8,256]{2,1,0:T(8,128)S(1)} %shard_map.95), kind=kLoop, calls=%fused_computation | loop fusion | bytes 32768 | tf_op jit(solution)/shard_map/squeeze | solution.py:631

commit v4 on v3

--- a/solution.py
+++ b/solution.py
@@ -55,7 +55,7 @@
     me = ix * ny + iy
 
     loads = [
-        pltpu.make_async_copy(src, dst, load_sem.at[j])
+        pltpu.make_async_copy(src, dst, load_sem.at[min(j, 1)])
         for j, (src, dst) in enumerate((
             (visc_in, visc_ref), (fric_in, fric_ref), (ground_in, ground_ref), (ice_in, ice_ref),
             (slide_in, slide_ref), (obs_in, obs_ref), (warm_in, warm_ref), (grad_in, grad_ref),
@@ -101,7 +101,7 @@
         dx, dy = DIRS[d]
         return pltpu.make_async_remote_copy(
             src_ref=src, dst_ref=dst,
-            send_sem=s_send.at[sem + d], recv_sem=s_recv.at[sem + OPPOSITE[d]],
+            send_sem=s_send.at[d], recv_sem=s_recv.at[sem + OPPOSITE[d]],
             device_id=(jnp.clip(ix + dx, 0, nx - 1), jnp.clip(iy + dy, 0, ny - 1)),
             device_id_type=MESH,
         )
@@ -157,8 +157,8 @@
             else:
                 fill(d_recv.at[d - 4])
 
-    for load in loads:
-        load.wait()
+    loads[0].wait()
+    pltpu.make_async_copy(visc_in.at[pl.ds(0, 8)], up.at[pl.ds(0, 8)], load_sem.at[1]).wait()
 
     ice = ice_ref[...].astype(jnp.float32)
     ground = ground_ref[...].astype(jnp.float32)
@@ -557,7 +557,7 @@
     )
 
     def send(j, c):
-        peer = lax.rem(2 * n - 1 - me + j, n)
+        peer = jnp.where(2 * me >= n, j, n - 1 - j)
 
         @pl.when(peer != me)
         def _():
@@ -570,7 +570,11 @@
             herald(r + 1)
     lax.fori_loop(0, n, send, 0, unroll=8)
     u0 = mine(back(full_y0, surface))
-    each("wait_send", for_x, along_x)
+    sent_rows = (levels + 2 + 3 * REACH + 2 * (REACH - 2) + 9 * (REACH - 1)) * (cols // 128) + 2 * REACH
+    for d in along_x:
+        @pl.when(exists(d))
+        def _():
+            copy(bot.at[0, pl.ds(0, sent_rows)], bot.at[0, pl.ds(0, sent_rows)], d, 0).wait_send()
     each("wait_send", for_y, along_y)
     each("wait_send", ("slant",), aslant)
     everybody.wait_recv()
@@ -621,8 +625,8 @@
                 f32(4, 3, rows, 128), f32(4, 3, rows, 128), f32(2, rows, 128), f32(2, 2, rows, 128),
                 f32(BASE + 8, 3 * rows, cols + 128),
                 f32(1, 128), f32(n, 1, 128),
-                pltpu.SemaphoreType.DMA((8,)),
-                pltpu.SemaphoreType.DMA((18,)), pltpu.SemaphoreType.DMA((18,)),
+                pltpu.SemaphoreType.DMA((2,)),
+                pltpu.SemaphoreType.DMA((8,)), pltpu.SemaphoreType.DMA((18,)),
                 pltpu.SemaphoreType.DMA, pltpu.SemaphoreType.DMA,
                 pltpu.SemaphoreType.REGULAR((max(1, (nx - 1).bit_length()), 2)),
             ],

time: 17.1 us -> 16.8 us (0.982)
  Pallas kernels: 15.7 us -> 15.4 us
    pallas_call x1, Pallas kernels: 15.7 us -> 15.4 us  [on_device(): pl.pallas_call(functools.partial(kernel, nx, ny), out_shape=f32(2, rows,...]
where the time goes in v4:
time: 16.8 us; the launch traced here: 16.7 us
  Pallas kernels  15.4 us (92%)
  between operations  0.64 us (4%)
  local copies, waits for them, and re-layouts  0.61 us (4%)
    pallas_call x1, Pallas kernels, on_device(): pl.pallas_call(functools.partial(kernel, nx, ny), out_shape=f32(2, rows,...  15.4 us
    squeeze x1, local copies, waits for them, and re-layouts, on_device(): return (out[0], out[1])  0.61 us

profile of v4, /device:TPU:0, one launch (start us, length us, event | category | flops | bytes accessed | tf_op | source)
XLA Modules:
  0.0 16.7 jit_solution(7887198748966487234)
XLA Ops:
  0.6 15.4 %shard_map.95 = f32[2,8,256]{2,1,0:T(8,128)S(1)} custom-call(f32[8,256]{1,0:T(8,128)} %grad_in.1, f32[8,256]{1,0:T(8,128)} %warm_in.1, f32[32,8,256]{2,1,0:T(8,128)} %visc_in.1, f32[8,256]{1,0:T(8,128)} %fric_in.1, f32[2,8,256]{2,1,0:T(8,128)} %slide_in.1, f32[8,256]{1,0:T(8,128)} %obs_in.1, s32[8,256]{1,0:T(8,128)} %ice_in.1, s32[8,256]{1,0:T(8,128)} %ground_in.1), custom_call_target="tpu_custom_call" | custom-call | tf_op jit(solution)/shard_map/pallas_call | solution.py:608
  16.1 0.6 %slice_bitcast_fusion = (f32[8,256]{1,0:T(8,128)}, f32[8,256]{1,0:T(8,128)}) fusion(f32[2,8,256]{2,1,0:T(8,128)S(1)} %shard_map.95), kind=kLoop, calls=%fused_computation | loop fusion | bytes 32768 | tf_op jit(solution)/shard_map/squeeze | solution.py:635

commit v5 on v4

--- a/solution.py
+++ b/solution.py
@@ -117,12 +117,12 @@
         return {
             "visc": lambda: copy(visc_ref.at[:, part(1), :], vx.at[:, part(1), :], d, 0),
             "slant": lambda: copy(d_send.at[d - 4], d_recv.at[o - 4], d, 0),
-            "edge": lambda: copy(e_send.at[:, part(1), :], ef.at[:, part(1), :], d, 8),
+            "edge": lambda: copy(e_send.at[:, part(1), :], ef.at[:, part(1), :], d, 0),
             "late": lambda: copy(q_send.at[side], q_recv.at[o - 2], d, 0),
-            "side": lambda: copy(px_send.at[:, part(REACH), :], px_recv.at[o, :, part(REACH), :], d, 10),
-            "wide": lambda: copy(a_send.at[:, part(REACH), :], a_recv.at[o, :, part(REACH), :], d, 12),
-            "less": lambda: copy(c_send.at[:, part(REACH - 2), :], c_recv.at[o, :, part(REACH - 2), :], d, 14),
-            "coef": lambda: copy(k_send.at[:, part(REACH - 1), :], k_recv.at[o, :, part(REACH - 1), :], d, 16),
+            "side": lambda: copy(px_send.at[:, part(REACH), :], px_recv.at[o, :, part(REACH), :], d, 8),
+            "wide": lambda: copy(a_send.at[:, part(REACH), :], a_recv.at[o, :, part(REACH), :], d, 10),
+            "less": lambda: copy(c_send.at[:, part(REACH - 2), :], c_recv.at[o, :, part(REACH - 2), :], d, 10),
+            "coef": lambda: copy(k_send.at[:, part(REACH - 1), :], k_recv.at[o, :, part(REACH - 1), :], d, 12),
         }[what]()
 
     along_x, along_y, aslant = (0, 1), (2, 3), (4, 5, 6, 7)
@@ -139,6 +139,13 @@
                         message(d, name).wait_send()
                     else:
                         message(d, name).start()
+
+    def arrive(sem, count):
+        block = bot.at[0, pl.ds(0, count * (cols // 128))]
+        for d in along_x:
+            @pl.when(exists(d))
+            def _():
+                copy(block, block, OPPOSITE[d], sem).wait_recv()
 
     def fill(ref, value=0.0):
         ref[...] = jnp.full(ref.shape, value, jnp.float32)
@@ -383,14 +390,15 @@
 
     last = rows - 1
     low, high = ready(own_row(0)), ready(own_row(last))
-    each("wait_recv", ("visc", "edge"), along_x)
+    arrive(0, levels + 2)
     respond(vx, upx, downx, bed_drag * ef[0], ef[1], far)
     below, above = ready(far_row(last)), ready(far_row(0))
     lines = {
         2 * rows - 1: across(high, above), 2 * rows: across(above, high),
         rows - 1: across(below, low), rows: across(low, below),
     }
-    each("wait_recv", ("side", "wide", "less"), along_x)
+    each("wait_recv", ("side",), along_x)
+    arrive(10, 3 * REACH + 2 * (REACH - 2))
     each("wait_recv", ("late",), along_y)
     low, high = ready(side_row(0)), ready(side_row(last))
     level_of = lax.rem(lane, levels)
@@ -626,7 +634,7 @@
                 f32(BASE + 8, 3 * rows, cols + 128),
                 f32(1, 128), f32(n, 1, 128),
                 pltpu.SemaphoreType.DMA((2,)),
-                pltpu.SemaphoreType.DMA((8,)), pltpu.SemaphoreType.DMA((18,)),
+                pltpu.SemaphoreType.DMA((8,)), pltpu.SemaphoreType.DMA((14,)),
                 pltpu.SemaphoreType.DMA, pltpu.SemaphoreType.DMA,
                 pltpu.SemaphoreType.REGULAR((max(1, (nx - 1).bit_length()), 2)),
             ],

time: 16.8 us -> 16.8 us (level)
  no operation moved by 1% of the time
where the time goes in v5:
time: 16.8 us; the launch traced here: 16.6 us
  Pallas kernels  15.4 us (92%)
  between operations  0.64 us (4%)
  local copies, waits for them, and re-layouts  0.61 us (4%)
    pallas_call x1, Pallas kernels, on_device(): pl.pallas_call(functools.partial(kernel, nx, ny), out_shape=f32(2, rows,...  15.4 us
    squeeze x1, local copies, waits for them, and re-layouts, on_device(): return (out[0], out[1])  0.61 us

profile of v5, /device:TPU:0, one launch (start us, length us, event | category | flops | bytes accessed | tf_op | source)
XLA Modules:
  0.0 16.6 jit_solution(11373817000779629029)
XLA Ops:
  0.6 15.4 %shard_map.95 = f32[2,8,256]{2,1,0:T(8,128)S(1)} custom-call(f32[8,256]{1,0:T(8,128)} %grad_in.1, f32[8,256]{1,0:T(8,128)} %warm_in.1, f32[32,8,256]{2,1,0:T(8,128)} %visc_in.1, f32[8,256]{1,0:T(8,128)} %fric_in.1, f32[2,8,256]{2,1,0:T(8,128)} %slide_in.1, f32[8,256]{1,0:T(8,128)} %obs_in.1, s32[8,256]{1,0:T(8,128)} %ice_in.1, s32[8,256]{1,0:T(8,128)} %ground_in.1), custom_call_target="tpu_custom_call" | custom-call | tf_op jit(solution)/shard_map/pallas_call | solution.py:616
  16.0 0.6 %slice_bitcast_fusion = (f32[8,256]{1,0:T(8,128)}, f32[8,256]{1,0:T(8,128)}) fusion(f32[2,8,256]{2,1,0:T(8,128)S(1)} %shard_map.95), kind=kLoop, calls=%fused_computation | loop fusion | bytes 32768 | tf_op jit(solution)/shard_map/squeeze | solution.py:643
